TPU v7x, 32 devices: a whole 2x2x4 slice. The times are simulated.
32 devices in a mesh: dp: 4 (over z), ctx: 4 (over y, core), tp: 2 (over x).
Axes of the slice: x: 2, y: 2, z: 4, core: 2. Of those that a mesh axis runs over, the one named last changes fastest.
Arguments:
- hidden: bfloat16 [4, 512, 4096], P('dp', 'ctx'), may hold values from -6 to 6
- query_heads: bfloat16 [4, 512, 4096], P('dp', 'ctx', 'tp'), may hold values from -6 to 6
- key_heads: bfloat16 [4, 512, 512], P('dp', 'ctx', 'tp'), may hold values from -6 to 6
- value_heads: bfloat16 [4, 512, 512], P('dp', 'ctx', 'tp'), may hold values from -6 to 6
- attention_out: bfloat16 [4, 512, 4096], P('dp', 'ctx', 'tp'), may hold values from -3 to 3
- output_grad: bfloat16 [4, 512, 4096], P('dp', 'ctx', 'tp'), may hold values from -3 to 3
- log_norm: float32 [4, 32, 512], P('dp', 'tp', 'ctx'), may hold values from -40 to 40, as said below
- block_order: int32 [8], replicated, may hold values from 0 to 7, as said below
- value_weight: bfloat16 [4096, 512], P(None, 'tp'), may hold values from -0.25 to 0.25
Outputs:
- query_grad: bfloat16 [4, 512, 4096], P('dp', 'ctx', 'tp')
- key_grad: bfloat16 [4, 512, 512], P('dp', 'ctx', 'tp')
- value_grad: bfloat16 [4, 512, 512], P('dp', 'ctx', 'tp')
- hidden_grad: bfloat16 [4, 512, 4096], P('dp', 'ctx', 'tp')
- weight_grad: float32 [4096, 512], P('ctx', 'tp')
Inputs may be any that keep to these rules, and one draw needn't show every extreme that they name: `block_order`: each of 0 to 7 once. log_norm is the log of the sum of exp(scores) over the keys visible to that row, so the probabilities of each row and head sum to one.
All inputs are finite; a program needn't handle non-finite values.
Results may differ from a plain program's by a relative error of at most 0.025.
Values may be sent and summed in bfloat16 or wider, within the bound.
A program may use at most 64 MiB of HBM per device.

v0:
```python
import math
import jax
import jax.numpy as jnp
from jax import lax
from jax.sharding import PartitionSpec as P

HD = 128
HQ = 32
KVH = 4


def block_positions(row_ids, block_order, block_len):
    labels = jnp.arange(block_order.shape[0], dtype=jnp.int32)
    picked = jnp.where((row_ids // block_len)[:, None] == labels[None, :], block_order[None, :], 0)
    return jnp.sum(picked, axis=1) * block_len + row_ids % block_len


def shards(
    hidden,
    query_heads,
    key_heads,
    value_heads,
    attention_out,
    output_grad,
    log_norm,
    block_order,
    value_weight,
):
    tokens = query_heads.shape[1]
    local_heads = key_heads.shape[2] // HD
    members = HQ // KVH
    block_len = tokens // 2
    cycle_size = lax.axis_size("ctx")
    cycle_rank = lax.axis_index("ctx")
    score_scale = HD ** (-0.5)
    local_rows = cycle_rank * tokens + jnp.arange(tokens, dtype=jnp.int32)
    query_pos = block_positions(local_rows, block_order, block_len)
    query_rows = query_heads[0].reshape(tokens, local_heads, members, HD)
    out_rows = attention_out[0].reshape(tokens, local_heads, members, HD)
    grad_rows = output_grad[0].reshape(tokens, local_heads, members, HD)
    row_delta = jnp.einsum(
        "tgjd,tgjd->gjt", grad_rows, out_rows, preferred_element_type=jnp.float32
    )
    norm_rows = log_norm[0].reshape(local_heads, members, tokens)

    def attend(running, key_block, value_block, block_first):
        key_count = key_block.shape[0]
        key_ids = block_first + jnp.arange(key_count, dtype=jnp.int32)
        key_pos = block_positions(key_ids, block_order, block_len)
        visible = key_pos[None, :] <= query_pos[:, None]
        acc_query, acc_key, acc_value = running
        scores = (
            jnp.einsum("tgjd,kgd->gjtk", query_rows, key_block, preferred_element_type=jnp.float32)
            * score_scale
        )
        shifted = jnp.where(visible[None, None], scores - norm_rows[:, :, :, None], -jnp.inf)
        probability = jnp.exp(shifted)
        weights = probability.astype(jnp.bfloat16)
        fresh_value = jnp.einsum(
            "gjtk,tgjd->kgd", weights, grad_rows, preferred_element_type=jnp.float32
        )
        through = jnp.einsum(
            "tgjd,kgd->gjtk", grad_rows, value_block, preferred_element_type=jnp.float32
        )
        slopes = (probability * (through - row_delta[:, :, :, None])).astype(jnp.bfloat16)
        acc_query = acc_query + jnp.einsum(
            "gjtk,kgd->tgjd", slopes, key_block, preferred_element_type=jnp.float32
        )
        fresh_key = jnp.einsum(
            "gjtk,tgjd->kgd", slopes, query_rows, preferred_element_type=jnp.float32
        )
        acc_key = lax.dynamic_update_slice_in_dim(
            acc_key,
            lax.dynamic_slice_in_dim(acc_key, block_first, key_count, 0) + fresh_key,
            block_first,
            0,
        )
        acc_value = lax.dynamic_update_slice_in_dim(
            acc_value,
            lax.dynamic_slice_in_dim(acc_value, block_first, key_count, 0) + fresh_value,
            block_first,
            0,
        )
        return (acc_query, acc_key, acc_value)

    def accumulate(running, pieces, first_row):
        key_piece, value_piece = pieces
        key_count = key_piece.shape[0]
        sub_width = math.gcd(key_count, 512)
        sub_turns = key_count // sub_width
        if sub_turns == 1:
            return attend(running, key_piece, value_piece, first_row)

        def advance(step_index, inner_state):
            offset = step_index * sub_width
            return attend(
                inner_state,
                lax.dynamic_slice_in_dim(key_piece, offset, sub_width, 0),
                lax.dynamic_slice_in_dim(value_piece, offset, sub_width, 0),
                first_row + offset,
            )

        return lax.fori_loop(0, sub_turns, advance, running)

    zeros_query = jnp.zeros((tokens, local_heads, members, HD), jnp.float32)
    zeros_pair = jnp.zeros((cycle_size * tokens, local_heads, HD), jnp.float32)
    key_local = key_heads[0].reshape(tokens, local_heads, HD)
    value_local = value_heads[0].reshape(tokens, local_heads, HD)
    acc_query, part_key, part_value = accumulate(
        (zeros_query, zeros_pair, zeros_pair),
        (
            lax.all_gather(key_local, "ctx", axis=0, tiled=True),
            lax.all_gather(value_local, "ctx", axis=0, tiled=True),
        ),
        jnp.int32(0),
    )
    own_key, own_value = (
        lax.psum_scatter(
            part_key.astype(jnp.bfloat16), "ctx", scatter_dimension=0, tiled=True
        ).astype(jnp.float32),
        lax.psum_scatter(
            part_value.astype(jnp.bfloat16), "ctx", scatter_dimension=0, tiled=True
        ).astype(jnp.float32),
    )
    query_grad = (
        (acc_query * score_scale)
        .astype(jnp.bfloat16)
        .reshape(1, tokens, local_heads * members * HD)
    )
    key_grad = (own_key * score_scale).astype(jnp.bfloat16).reshape(1, tokens, local_heads * HD)
    value_grad = own_value.astype(jnp.bfloat16).reshape(1, tokens, local_heads * HD)
    value_rows = value_grad[0]
    inputs = hidden[0]
    partial_term = jnp.einsum("td,te->de", inputs, value_rows, preferred_element_type=jnp.float32)
    row_share = lax.psum_scatter(
        lax.optimization_barrier(partial_term.astype(jnp.bfloat16))
        .astype(jnp.float32)
        .astype(jnp.bfloat16),
        "ctx",
        scatter_dimension=0,
        tiled=True,
    )
    summed_rows = lax.psum(row_share, "dp").astype(jnp.float32)
    token_norm = (lax.axis_size("dp") * cycle_size * tokens) ** (-0.5)
    weight_grad = summed_rows * token_norm
    partial_value = jnp.einsum(
        "te,de->td", value_rows, value_weight, preferred_element_type=jnp.float32
    )
    summed = lax.psum_scatter(
        partial_value.astype(jnp.bfloat16), "tp", scatter_dimension=1, tiled=True
    ).astype(jnp.float32)
    hidden_grad = summed.astype(jnp.bfloat16).reshape(1, tokens, summed.shape[1])
    return (query_grad, key_grad, value_grad, hidden_grad, weight_grad)


def solution(mesh):
    placed = (
        P("dp", "ctx", None),
        P("dp", "ctx", "tp"),
        P("dp", "ctx", "tp"),
        P("dp", "ctx", "tp"),
        P("dp", "ctx", "tp"),
        P("dp", "ctx", "tp"),
        P("dp", "tp", "ctx"),
        P(),
        P(None, "tp"),
    )
    return jax.shard_map(
        shards,
        mesh=mesh,
        in_specs=placed,
        out_specs=(
            P("dp", "ctx", "tp"),
            P("dp", "ctx", "tp"),
            P("dp", "ctx", "tp"),
            P("dp", "ctx", "tp"),
            P("ctx", "tp"),
        ),
        check_vma=False,
    )
```

profile of v0, /device:TPU:0, one launch (start us, length us, event | category | flops | bytes accessed | tf_op | source)
XLA Modules:
  0.0 174.6 jit_solution(1316045915267573734)
XLA Ops:
  7.2 0.0 copy-start
  7.2 0.0 copy-start.5
  7.2 0.0 reduce-scatter.7.cloned.1.call-start
  7.3 0.9 select_reduce_fusion.1
  8.2 0.7 select_reduce_fusion
  8.9 0.9 copy.39
  9.9 0.1 copy.40
  10.0 7.3 %all_gather.6 = bf16[512,2,128]{2,0,1:T(8,128)(2,1)S(1)} all-gather(bf16[128,2,128]{2,0,1:T(8,128)(2,1)S(1)} %copy.40), channel_id=1, replica_groups=mesh['dp'=4,'ctx'=4,'tp'=2] {'ctx'}, dimensions={0}, use_global_device_ids=true | all-gather | bytes 327680 | tf_op jit(solution)/shard_map/all_gather | solution.py:112
  17.2 1.1 copy.72
  18.4 1.1 copy.73
  19.5 0.1 broadcast_compare_fusion
  19.7 0.0 copy-start.4
  19.7 0.7 fusion.26
  20.4 0.0 copy-start.1
  20.4 1.9 %copy-done.1 = f32[2,512,128,8]{2,1,3,0:T(8,128)} copy-done((f32[2,512,128,8]{2,1,3,0:T(8,128)}, f32[2,512,128,8]{2,1,3,0:T(8,128)S(1)}, u32[]{:S(2)}) %copy-start.1) | copy-done | bytes 4194328
  22.3 0.0 copy-done.5
  22.3 1.7 %fusion.17 = bf16[512,2,128]{2,0,1:T(8,128)(2,1)} fusion(f32[2,512,128,8]{2,1,3,0:T(8,128)S(1)} %fusion.26, f32[2,8,128]{2,1,0:T(8,128)S(1)} %bitcast.109, pred[128,512]{0,1:T(8,128)(4,1)S(1)} %broadcast_compare_fusion, bf16[128,2,8,128]{3,2,1,0:T(8,128)(2,1)S(1)} %bitcast.94), kind=kOutput, calls=%fused_computation.18 | convolution fusion | flops 272760832 | bytes 5054464 | tf_op jit(solution)/shard_map/gjtk,tgjd->kgd/dot_general | solution.py:59
  24.1 0.0 copy-done.4
  24.1 0.0 copy-start.3
  24.1 0.0 reduce-scatter.7.cloned.1.call-update
  24.1 0.0 reduce-scatter.11.cloned.1.call-start
  24.2 21.4 %reduce-scatter.7.cloned.1.call-done = bf16[128,2,128]{2,0,1:T(8,128)(2,1)} async-done(((bf16[512,2,128]{2,0,1:T(8,128)(2,1)}), bf16[128,2,128]{2,0,1:T(8,128)(2,1)}) %reduce-scatter.7.cloned.1.call-update) | async-done | bytes 65552 | tf_op jit(solution)/shard_map/reduce_scatter | solution.py:121
  45.6 0.9 copy.50
  46.6 3.3 %fusion = bf16[4096,256]{0,1:T(8,128)(2,1)} fusion(bf16[128,256]{0,1:T(8,128)(2,1)S(1)} %bitcast.99, bf16[1,128,4096]{2,1,0:T(8,128)(2,1)} %param.9), kind=kOutput, calls=%fused_computation.1 | convolution fusion | flops 269484032 | bytes 3211264 | tf_op jit(solution)/shard_map/td,te->de/dot_general | solution.py:134
  49.8 0.0 reduce-scatter.11.cloned.1.call-update
  49.8 0.0 reduce-scatter.5.cloned.1.call-start
  49.9 0.0 copy-done.3
  49.9 0.7 copy.42
  50.6 0.9 copy.43
  51.6 1.2 copy.74
  52.8 1.1 fusion.22
  53.9 1.0 copy.64
  54.8 5.8 %all_gather.7 = bf16[512,2,128]{2,0,1:T(8,128)(2,1)S(1)} all-gather(bf16[128,2,128]{2,0,1:T(8,128)(2,1)S(1)} %copy.43), channel_id=1, replica_groups=mesh['dp'=4,'ctx'=4,'tp'=2] {'ctx'}, dimensions={0}, use_global_device_ids=true | all-gather | bytes 327680 | tf_op jit(solution)/shard_map/all_gather | solution.py:113
  60.6 3.6 %fusion.2 = bf16[2,8,128,512]{2,3,1,0:T(8,128)(2,1)S(1)} fusion(f32[2,512,128,8]{2,1,3,0:T(8,128)} %copy-done.1, f32[2,8,128]{2,1,0:T(8,128)S(1)} %copy.64, f32[2,8,128]{2,1,0:T(8,128)S(1)} %bitcast.110, pred[128,512]{0,1:T(8,128)(4,1)} %copy-done.4, bf16[128,2,8,128]{3,2,1,0:T(8,128)(2,1)S(1)} %bitcast.96, bf16[512,2,128]{2,0,1:T(8,128)(2,1)S(1)} %all_gather.7), kind=kOutput, calls=%fused_computation.5 | convolution fusion | flops 274726912 | bytes 7159808 | tf_op jit(solution)/shard_map/tgjd,kgd->gjtk/dot_general | solution.py:62
  64.2 0.0 copy-start.2
  64.2 1.3 copy-done.2
  65.6 1.4 fusion.20
  67.0 0.0 reduce-scatter.5.cloned.1.call-update
  67.0 0.0 all-reduce.2.cloned.1.call-start
  67.1 14.1 %reduce-scatter.11.cloned.1.call-done = bf16[1024,256]{0,1:T(8,128)(2,1)} async-done(((bf16[4096,256]{0,1:T(8,128)(2,1)}), bf16[1024,256]{0,1:T(8,128)(2,1)}) %reduce-scatter.11.cloned.1.call-update) | async-done | bytes 524304 | tf_op jit(solution)/shard_map/reduce_scatter | solution.py:135
  81.2 0.0 all-reduce.2.cloned.1.call-update
  81.2 0.0 reduce-scatter.9.cloned.1.call-start
  81.3 0.0 copy-done
  81.3 1.8 %convolution_convert_fusion.1 = bf16[128,4096]{1,0:T(8,128)(2,1)} fusion(bf16[128,256]{0,1:T(8,128)(2,1)S(1)} %bitcast.100, bf16[4096,256]{1,0:T(8,128)(2,1)S(1)} %copy-done), kind=kOutput, calls=%fused_computation.2 | convolution fusion | flops 268959744 | bytes 3211264 | tf_op jit(solution)/shard_map/te,de->td/dot_general | solution.py:146
  83.1 0.0 reduce-scatter.9.cloned.1.call-update
  83.1 2.1 %fusion.9 = bf16[2,8,128,128]{2,3,1,0:T(8,128)(2,1)S(1)} fusion(bf16[2,8,128,512]{2,3,1,0:T(8,128)(2,1)} %copy-done.2, bf16[512,2,128]{2,0,1:T(8,128)(2,1)S(1)} %all_gather.6), kind=kOutput, calls=%fused_computation.13 | convolution fusion | flops 268959744 | bytes 2883584 | tf_op jit(solution)/shard_map/gjtk,kgd->tgjd/dot_general | solution.py:66
  85.2 1.0 copy.52
  86.2 18.1 %reduce-scatter.5.cloned.1.call-done = bf16[128,2,128]{2,0,1:T(8,128)(2,1)} async-done(((bf16[512,2,128]{2,0,1:T(8,128)(2,1)}), bf16[128,2,128]{2,0,1:T(8,128)(2,1)}) %reduce-scatter.5.cloned.1.call-update) | async-done | bytes 65552 | tf_op jit(solution)/shard_map/reduce_scatter | solution.py:118
  104.3 0.9 multiply_convert_fusion
  105.2 0.1 copy.48
  105.3 0.7 copy.53
  106.0 0.7 copy.54
  106.8 38.4 %all-reduce.2.cloned.1.call-done = bf16[1024,256]{0,1:T(8,128)(2,1)} async-done(((bf16[1024,256]{0,1:T(8,128)(2,1)}), bf16[1024,256]{0,1:T(8,128)(2,1)}) %all-reduce.2.cloned.1.call-update) | async-done | bytes 524304 | tf_op jit(solution)/shard_map/psum | solution.py:143
  145.2 1.2 convert_multiply_fusion.1
  146.4 1.3 copy.55
  147.7 20.4 %reduce-scatter.9.cloned.1.call-done = bf16[128,2048]{1,0:T(8,128)(2,1)} async-done(((bf16[128,4096]{1,0:T(8,128)(2,1)}), bf16[128,2048]{1,0:T(8,128)(2,1)}) %reduce-scatter.9.cloned.1.call-update) | async-done | bytes 524304 | tf_op jit(solution)/shard_map/reduce_scatter | solution.py:149
  (4 shorter events, 0.0 us)
Async XLA Ops:
  7.2 74.1 %copy-start = (bf16[4096,256]{1,0:T(8,128)(2,1)S(1)}, bf16[4096,256]{1,0:T(8,128)(2,1)}, u32[]{:S(2)}) copy-start(bf16[4096,256]{1,0:T(8,128)(2,1)} %param.17) | copy-start | bytes 6291460
  7.2 15.2 %copy-start.5 = (f32[1,16,128]{2,1,0:T(8,128)S(1)}, f32[1,16,128]{2,1,0:T(8,128)}, u32[]{:S(2)}) copy-start(f32[1,16,128]{2,1,0:T(8,128)} %param.15) | copy-start | bytes 24580
  7.2 38.4 %reduce-scatter.7.cloned.1.call-start = ((), (), s32[]{:S(2)}) async-start(), calls=%async_computation.5 | async-start | bytes 327680 | tf_op jit(solution)/shard_map/reduce_scatter | solution.py:121
  19.7 4.4 %copy-start.4 = (pred[128,512]{0,1:T(8,128)(4,1)}, pred[128,512]{0,1:T(8,128)(4,1)S(1)}, u32[]{:S(2)}) copy-start(pred[128,512]{0,1:T(8,128)(4,1)S(1)} %broadcast_compare_fusion) | copy-start | bytes 196612
  20.4 1.9 %copy-start.1 = (f32[2,512,128,8]{2,1,3,0:T(8,128)}, f32[2,512,128,8]{2,1,3,0:T(8,128)S(1)}, u32[]{:S(2)}) copy-start(f32[2,512,128,8]{2,1,3,0:T(8,128)S(1)} %fusion.26) | copy-start | bytes 12582916
  24.1 25.8 %copy-start.3 = (bf16[1,128,256]{2,1,0:T(8,128)(2,1)S(1)}, bf16[1,128,256]{2,1,0:T(8,128)(2,1)}, u32[]{:S(2)}) copy-start(bf16[1,128,256]{2,1,0:T(8,128)(2,1)} %param.12) | copy-start | bytes 196612
  24.1 57.1 %reduce-scatter.11.cloned.1.call-start = ((), (), s32[]{:S(2)}) async-start(), calls=%async_computation.7 | async-start | bytes 2621440 | tf_op jit(solution)/shard_map/reduce_scatter | solution.py:135
  49.8 54.5 %reduce-scatter.5.cloned.1.call-start = ((), (), s32[]{:S(2)}) async-start(), calls=%async_computation.4 | async-start | bytes 327680 | tf_op jit(solution)/shard_map/reduce_scatter | solution.py:118
  64.2 1.4 copy-start.2
  67.0 78.2 %all-reduce.2.cloned.1.call-start = ((), (), s32[]{:S(2)}) async-start(), calls=%async_computation.8 | async-start | bytes 1048576 | tf_op jit(solution)/shard_map/psum | solution.py:143
  81.2 86.9 %reduce-scatter.9.cloned.1.call-start = ((), (), s32[]{:S(2)}) async-start(), calls=%async_computation.6 | async-start | bytes 1572864 | tf_op jit(solution)/shard_map/reduce_scatter | solution.py:149
Sparse Core Ops, SparseCore 0:
  24.2 21.3 reduce-scatter.6
  50.0 31.1 reduce-scatter.10
  84.2 20.0 reduce-scatter.4
  106.5 38.6 all-reduce.1
  147.9 20.1 reduce-scatter.8
where the time goes:
time: 175 us
  waiting for transfers between devices  113 us (65%)
  local copies, waits for them, and re-layouts  15.3 us (9%)
  matrix products  14.6 us (8%)
  between operations  14 us (8%)
  blocking collectives  13 us (7%)
  other arithmetic  4.91 us (3%)
    psum x1, waiting for transfers between devices, shards(): summed_rows = lax.psum(row_share, 'dp').astype(jnp.float32)  38.4 us
    reduce_scatter x1, waiting for transfers between devices, shards(): lax.psum_scatter(part_value.astype(jnp.bfloat16), 'ctx', scatter_dimensio...  21.4 us
    reduce_scatter x1, waiting for transfers between devices, shards(): lax.psum_scatter(partial_value.astype(jnp.bfloat16), 'tp', scatter_dimens...  20.4 us
    reduce_scatter x1, waiting for transfers between devices, shards(): lax.psum_scatter(part_key.astype(jnp.bfloat16), 'ctx', scatter_dimension=...  18.1 us
    reduce_scatter x1, waiting for transfers between devices, shards(): lax.psum_scatter(lax.optimization_barrier(partial_term.astype(jnp.bfloat1...  14.1 us
    unnamed x21, local copies, waits for them, and re-layouts  12.2 us
    all_gather x1, blocking collectives, shards(): lax.all_gather(key_local, 'ctx', axis=0, tiled=True)  7.25 us
    all_gather x1, blocking collectives, shards(): lax.all_gather(value_local, 'ctx', axis=0, tiled=True)  5.78 us
  transfers between devices with their start and end apart: 5, of which 5 were waited for; matrix products, arithmetic and copies ran while one was open for 11% of the time, Pallas kernels for 0%

commit v1 on v0

--- a/solution.py
+++ b/solution.py
@@ -26,6 +26,11 @@
     block_order,
     value_weight,
 ):
+
+    def lay_floor(t0, ax_name):
+        field_out = lax.all_gather(t0, axis_name=ax_name)
+        return jnp.sum(field_out, axis=0)
+
     tokens = query_heads.shape[1]
     local_heads = key_heads.shape[2] // HD
     members = HQ // KVH
@@ -140,7 +145,7 @@
         scatter_dimension=0,
         tiled=True,
     )
-    summed_rows = lax.psum(row_share, "dp").astype(jnp.float32)
+    summed_rows = lay_floor(row_share, "dp").astype(jnp.float32)
     token_norm = (lax.axis_size("dp") * cycle_size * tokens) ** (-0.5)
     weight_grad = summed_rows * token_norm
     partial_value = jnp.einsum(

time: 175 us -> 181 us (1.034)
  waiting for transfers between devices: 113 us -> 108 us
  other arithmetic: 4.91 us -> 9.85 us
  local copies, waits for them, and re-layouts: 15.3 us -> 19.8 us
    all_gather x0 -> x1, waiting for transfers between devices: none -> 44.6 us  [lay_floor(): field_out = lax.all_gather(t0, axis_name=ax_name)]
    psum x1 -> x0, waiting for transfers between devices: 38.4 us -> none  [shards(): summed_rows = lax.psum(row_share, 'dp').astype(jnp.float32)]
    reduce_scatter x1, waiting for transfers between devices: 20.4 us -> 9.99 us  [shards(): lax.psum_scatter(partial_value.astype(jnp.bfloat16), 'tp', scatter_dimens...]
    reduce_sum x0 -> x1, other arithmetic: none -> 4.93 us  [lay_floor(): return jnp.sum(field_out, axis=0)]
    all_gather x0 -> x1, local copies, waits for them, and re-layouts: none -> 4.51 us  [lay_floor(): field_out = lax.all_gather(t0, axis_name=ax_name)]
  transfers between devices with their start and end apart: 5 -> 5, of which waited for: 5 -> 5; matrix products, arithmetic and copies ran while one was open for 11% -> 16% of each run, Pallas kernels for 0% -> 0%
where the time goes in v1:
time: 181 us; the launch traced here: 180 us
  waiting for transfers between devices  108 us (60%)
  local copies, waits for them, and re-layouts  19.8 us (11%)
  matrix products  14.6 us (8%)
  between operations  14 us (8%)
  blocking collectives  13 us (7%)
  other arithmetic  9.85 us (5%)
    all_gather x1, waiting for transfers between devices, lay_floor(): field_out = lax.all_gather(t0, axis_name=ax_name)  44.6 us
    reduce_scatter x1, waiting for transfers between devices, shards(): lax.psum_scatter(part_value.astype(jnp.bfloat16), 'ctx', scatter_dimensio...  21.4 us
    reduce_scatter x1, waiting for transfers between devices, shards(): lax.psum_scatter(part_key.astype(jnp.bfloat16), 'ctx', scatter_dimension=...  18.1 us
    reduce_scatter x1, waiting for transfers between devices, shards(): lax.psum_scatter(lax.optimization_barrier(partial_term.astype(jnp.bfloat1...  14.2 us
    unnamed x21, local copies, waits for them, and re-layouts  12.1 us
    reduce_scatter x1, waiting for transfers between devices, shards(): lax.psum_scatter(partial_value.astype(jnp.bfloat16), 'tp', scatter_dimens...  9.99 us
    all_gather x1, blocking collectives, shards(): lax.all_gather(key_local, 'ctx', axis=0, tiled=True)  7.25 us
    all_gather x1, blocking collectives, shards(): lax.all_gather(value_local, 'ctx', axis=0, tiled=True)  5.78 us
  transfers between devices with their start and end apart: 5, of which 5 were waited for; matrix products, arithmetic and copies ran while one was open for 16% of the time, Pallas kernels for 0%

profile of v1, /device:TPU:0, one launch (start us, length us, event | category | flops | bytes accessed | tf_op | source)
XLA Modules:
  0.0 179.8 jit_solution(16315202299684812930)
XLA Ops:
  7.2 0.0 copy-start
  7.2 0.0 copy-start.5
  7.2 0.0 reduce-scatter.7.cloned.1.call-start
  7.3 0.9 select_reduce_fusion.1
  8.2 0.7 select_reduce_fusion
  8.9 0.9 copy.54
  9.9 0.1 copy.55
  10.0 7.3 %all_gather.12 = bf16[512,2,128]{2,0,1:T(8,128)(2,1)S(1)} all-gather(bf16[128,2,128]{2,0,1:T(8,128)(2,1)S(1)} %copy.55), channel_id=1, replica_groups=mesh['dp'=4,'ctx'=4,'tp'=2] {'ctx'}, dimensions={0}, use_global_device_ids=true | all-gather | bytes 327680 | tf_op jit(solution)/shard_map/all_gather | solution.py:117
  17.2 1.1 copy.87
  18.4 1.1 copy.88
  19.5 0.1 broadcast_compare_fusion
  19.7 0.0 copy-start.4
  19.7 0.7 fusion.26
  20.4 0.0 copy-start.1
  20.4 0.0 copy-done.4
  20.4 1.9 %copy-done.1 = f32[2,512,128,8]{2,1,3,0:T(8,128)} copy-done((f32[2,512,128,8]{2,1,3,0:T(8,128)}, f32[2,512,128,8]{2,1,3,0:T(8,128)S(1)}, u32[]{:S(2)}) %copy-start.1) | copy-done | bytes 4194328
  22.3 0.0 copy-done.5
  22.3 1.7 fusion.17
  24.1 0.0 copy-start.3
  24.1 0.0 reduce-scatter.7.cloned.1.call-update
  24.1 0.0 reduce-scatter.11.cloned.1.call-start
  24.2 21.4 %reduce-scatter.7.cloned.1.call-done = bf16[128,2,128]{2,0,1:T(8,128)(2,1)} async-done(((bf16[512,2,128]{2,0,1:T(8,128)(2,1)}), bf16[128,2,128]{2,0,1:T(8,128)(2,1)}) %reduce-scatter.7.cloned.1.call-update) | async-done | bytes 65552 | tf_op jit(solution)/shard_map/reduce_scatter | solution.py:126
  45.6 0.9 copy.65
  46.6 3.3 %fusion = bf16[4096,256]{0,1:T(8,128)(2,1)} fusion(bf16[128,256]{0,1:T(8,128)(2,1)S(1)} %bitcast.101, bf16[1,128,4096]{2,1,0:T(8,128)(2,1)} %param.9), kind=kOutput, calls=%fused_computation.1 | convolution fusion | flops 269484032 | bytes 3211264 | tf_op jit(solution)/shard_map/td,te->de/dot_general | solution.py:139
  49.8 0.0 reduce-scatter.11.cloned.1.call-update
  49.8 0.0 reduce-scatter.5.cloned.1.call-start
  49.9 0.0 copy-done.3
  49.9 0.7 copy.57
  50.6 0.9 copy.58
  51.6 1.2 copy.89
  52.7 1.1 fusion.22
  53.9 1.0 copy.79
  54.8 5.8 %all_gather.13 = bf16[512,2,128]{2,0,1:T(8,128)(2,1)S(1)} all-gather(bf16[128,2,128]{2,0,1:T(8,128)(2,1)S(1)} %copy.58), channel_id=1, replica_groups=mesh['dp'=4,'ctx'=4,'tp'=2] {'ctx'}, dimensions={0}, use_global_device_ids=true | all-gather | bytes 327680 | tf_op jit(solution)/shard_map/all_gather | solution.py:118
  60.6 3.6 %fusion.2 = bf16[2,8,128,512]{2,3,1,0:T(8,128)(2,1)S(1)} fusion(f32[2,512,128,8]{2,1,3,0:T(8,128)} %copy-done.1, f32[2,8,128]{2,1,0:T(8,128)S(1)} %copy.79, f32[2,8,128]{2,1,0:T(8,128)S(1)} %bitcast.112, pred[128,512]{0,1:T(8,128)(4,1)} %copy-done.4, bf16[128,2,8,128]{3,2,1,0:T(8,128)(2,1)S(1)} %bitcast.98, bf16[512,2,128]{2,0,1:T(8,128)(2,1)S(1)} %all_gather.13), kind=kOutput, calls=%fused_computation.5 | convolution fusion | flops 274726912 | bytes 7159808 | tf_op jit(solution)/shard_map/tgjd,kgd->gjtk/dot_general | solution.py:67
  64.2 0.0 copy-start.2
  64.2 1.3 copy-done.2
  65.5 1.4 fusion.20
  66.9 0.0 reduce-scatter.5.cloned.1.call-update
  66.9 0.0 all-gather.3.cloned.1.call-start
  67.0 14.2 %reduce-scatter.11.cloned.1.call-done = bf16[1024,256]{0,1:T(8,128)(2,1)} async-done(((bf16[4096,256]{0,1:T(8,128)(2,1)}), bf16[1024,256]{0,1:T(8,128)(2,1)}) %reduce-scatter.11.cloned.1.call-update) | async-done | bytes 524304 | tf_op jit(solution)/shard_map/reduce_scatter | solution.py:140
  81.2 0.0 all-gather.3.cloned.1.call-update
  81.2 0.0 reduce-scatter.9.cloned.1.call-start
  81.2 0.0 copy-done
  81.3 1.8 convolution_convert_fusion.1
  83.0 0.0 reduce-scatter.9.cloned.1.call-update
  83.1 2.1 %fusion.9 = bf16[2,8,128,128]{2,3,1,0:T(8,128)(2,1)S(1)} fusion(bf16[2,8,128,512]{2,3,1,0:T(8,128)(2,1)} %copy-done.2, bf16[512,2,128]{2,0,1:T(8,128)(2,1)S(1)} %all_gather.12), kind=kOutput, calls=%fused_computation.13 | convolution fusion | flops 268959744 | bytes 2883584 | tf_op jit(solution)/shard_map/gjtk,kgd->tgjd/dot_general | solution.py:71
  85.2 1.0 copy.67
  86.2 18.1 %reduce-scatter.5.cloned.1.call-done = bf16[128,2,128]{2,0,1:T(8,128)(2,1)} async-done(((bf16[512,2,128]{2,0,1:T(8,128)(2,1)}), bf16[128,2,128]{2,0,1:T(8,128)(2,1)}) %reduce-scatter.5.cloned.1.call-update) | async-done | bytes 65552 | tf_op jit(solution)/shard_map/reduce_scatter | solution.py:123
  104.3 0.9 multiply_convert_fusion
  105.2 0.1 copy.63
  105.3 0.7 copy.68
  106.0 0.7 copy.69
  106.8 44.6 %all-gather.3.cloned.1.call-done = bf16[4096,256]{0,1:T(8,128)(2,1)} async-done(((bf16[1024,256]{0,1:T(8,128)(2,1)}), bf16[4096,256]{0,1:T(8,128)(2,1)}) %all-gather.3.cloned.1.call-update) | async-done | bytes 2097168 | tf_op jit(solution)/shard_map/all_gather | solution.py:31
  151.4 4.5 %reshape.118 = bf16[4,1024,256]{1,0,2:T(4,128)(2,1)} reshape(bf16[4096,256]{0,1:T(8,128)(2,1)} %all-gather.3.cloned.1.call-done) | data formatting | bytes 4194304 | tf_op jit(solution)/shard_map/all_gather | solution.py:31
  155.9 4.9 %reduce_sum.32 = bf16[1024,256]{0,1:T(8,128)(2,1)} reduce(bf16[4,1024,256]{1,0,2:T(4,128)(2,1)} %reshape.118, bf16[]{:T(256)} %constant.68.clone.1), dimensions={0}, to_apply=%region_6.7 | reduce | flops 786432 | bytes 2621442 | tf_op jit(solution)/shard_map/reduce_sum | solution.py:32
  160.9 1.2 convert_multiply_fusion.1
  162.0 1.3 copy.70
  163.3 10.0 %reduce-scatter.9.cloned.1.call-done = bf16[128,2048]{1,0:T(8,128)(2,1)} async-done(((bf16[128,4096]{1,0:T(8,128)(2,1)}), bf16[128,2048]{1,0:T(8,128)(2,1)}) %reduce-scatter.9.cloned.1.call-update) | async-done | bytes 524304 | tf_op jit(solution)/shard_map/reduce_scatter | solution.py:154
  (4 shorter events, 0.0 us)
Async XLA Ops:
  7.2 74.1 %copy-start = (bf16[4096,256]{1,0:T(8,128)(2,1)S(1)}, bf16[4096,256]{1,0:T(8,128)(2,1)}, u32[]{:S(2)}) copy-start(bf16[4096,256]{1,0:T(8,128)(2,1)} %param.17) | copy-start | bytes 6291460
  7.2 15.2 %copy-start.5 = (f32[1,16,128]{2,1,0:T(8,128)S(1)}, f32[1,16,128]{2,1,0:T(8,128)}, u32[]{:S(2)}) copy-start(f32[1,16,128]{2,1,0:T(8,128)} %param.15) | copy-start | bytes 24580
  7.2 38.4 %reduce-scatter.7.cloned.1.call-start = ((), (), s32[]{:S(2)}) async-start(), calls=%async_computation.5 | async-start | bytes 327680 | tf_op jit(solution)/shard_map/reduce_scatter | solution.py:126
  19.7 0.7 copy-start.4
  20.4 1.9 %copy-start.1 = (f32[2,512,128,8]{2,1,3,0:T(8,128)}, f32[2,512,128,8]{2,1,3,0:T(8,128)S(1)}, u32[]{:S(2)}) copy-start(f32[2,512,128,8]{2,1,3,0:T(8,128)S(1)} %fusion.26) | copy-start | bytes 12582916
  24.1 25.8 %copy-start.3 = (bf16[1,128,256]{2,1,0:T(8,128)(2,1)S(1)}, bf16[1,128,256]{2,1,0:T(8,128)(2,1)}, u32[]{:S(2)}) copy-start(bf16[1,128,256]{2,1,0:T(8,128)(2,1)} %param.12) | copy-start | bytes 196612
  24.1 57.0 %reduce-scatter.11.cloned.1.call-start = ((), (), s32[]{:S(2)}) async-start(), calls=%async_computation.7 | async-start | bytes 2621440 | tf_op jit(solution)/shard_map/reduce_scatter | solution.py:140
  49.8 54.5 %reduce-scatter.5.cloned.1.call-start = ((), (), s32[]{:S(2)}) async-start(), calls=%async_computation.4 | async-start | bytes 327680 | tf_op jit(solution)/shard_map/reduce_scatter | solution.py:123
  64.2 1.3 copy-start.2
  66.9 84.5 %all-gather.3.cloned.1.call-start = ((), (), s32[]{:S(2)}) async-start(), calls=%async_computation.8 | async-start | bytes 2621440 | tf_op jit(solution)/shard_map/all_gather | solution.py:31
  81.2 92.1 %reduce-scatter.9.cloned.1.call-start = ((), (), s32[]{:S(2)}) async-start(), calls=%async_computation.6 | async-start | bytes 1572864 | tf_op jit(solution)/shard_map/reduce_scatter | solution.py:154
Sparse Core Ops, SparseCore 0:
  24.2 21.3 reduce-scatter.6
  50.0 31.1 reduce-scatter.10
  84.2 20.0 reduce-scatter.4
  105.7 45.6 all-gather.2
  154.1 19.1 reduce-scatter.8
